TPU v7x, 256 devices: a whole 4x4x8 slice. The times are simulated.
256 devices in a mesh: group: 8 (over z), dom: 32 (over y, x, core).
Axes of the slice: x: 4, y: 4, z: 8, core: 2. Of those that a mesh axis runs over, the one named last changes fastest.
Arguments:
- features: bfloat16 [131072, 128], P(('group', 'dom')), may hold values from -6 to 6
- cotangent: bfloat16 [131072, 128], P(('group', 'dom')), may hold values from -6 to 6
- fine_send: int32 [8192, 16], P(('group', 'dom')), may hold values from 0 to 512, as said below
- fine_rim: int32 [512, 128], P(('group', 'dom')), may hold values from 0 to 511
- fine_src: int32 [1048576], P(('group', 'dom')), may hold values from 0 to 1279, as said below
- fine_dst: int32 [1048576], P(('group', 'dom')), may hold values from 0 to 511
- fine_pool: int32 [131072], P(('group', 'dom')), may hold values from 0 to 1023, as said below
- coarse_send: int32 [8192, 4], P(('group', 'dom')), may hold values from 0 to 32, as said below
- coarse_src: int32 [65536], P(('group', 'dom')), may hold values from 0 to 159, as said below
- coarse_dst: int32 [65536], P(('group', 'dom')), may hold values from 0 to 31
- coarse_pool: int32 [8192], P(('group', 'dom')), may hold values from 0 to 511
- w_send: bfloat16 [128, 128], replicated, may hold values from -0.5 to 0.5
- w_recv: bfloat16 [128, 128], replicated, may hold values from -0.5 to 0.5
- w_node: bfloat16 [128, 128], replicated, may hold values from -0.5 to 0.5
- v_send: bfloat16 [128, 128], replicated, may hold values from -0.5 to 0.5
- v_recv: bfloat16 [128, 128], replicated, may hold values from -0.5 to 0.5
- v_node: bfloat16 [128, 128], replicated, may hold values from -0.5 to 0.5
- w_top: bfloat16 [128, 128], replicated, may hold values from -0.5 to 0.5
Outputs:
- flow: bfloat16 [131072, 128], P(('group', 'dom'))
- grad_features: float32 [131072, 128], P(('group', 'dom'))
- grad_send: float32 [128, 128], replicated
Inputs may be any that keep to these rules, and one draw needn't show every extreme that they name: `fine_send`: each device holds 32 rows of 16: row p lists own node rows for the device with dom index p of its group; the value 512 marks an empty slot, live slots come first, and three rows of every device are full. `fine_rim`: each device holds two rows: the first go to the previous group's device of the same dom index, the second to the next group's. `fine_src`: index into the device's extended rows: its 512 nodes, 512 rows from its group in dom order, 128 rows from the previous group, 128 from the next. `fine_pool`: coarse node numbered within the node's group. `coarse_send`: as fine_send with 4 slots a row and 32 marking an empty slot. `coarse_src`: index into the device's coarse rows, then 32 * 4 rows from its group in dom order.
All inputs are finite; a program needn't handle non-finite values.
Results may differ from a plain program's by a relative error of at most 0.025.
Values may be sent and summed in bfloat16 or wider, within the bound.
A program may use at most 64 MiB of HBM per device.

v0:
```python
import jax
import jax.numpy as jnp
from jax import lax
from jax.sharding import Mesh
from jax.sharding import PartitionSpec as P

NCC = 512
DOM = ("dom_0", "dom_1", "dom_2")
GROUP_DOM = ("group", "dom_0", "dom_1", "dom_2")


def with_halo(block, sides, width):
    for axis, dim in sides:
        count = lax.axis_size(axis)
        forward = [(i, i + 1) for i in range(count - 1)]
        backward = [(target, source) for source, target in forward]
        low = lax.ppermute(
            lax.slice_in_dim(block, block.shape[dim] - width, None, axis=dim), axis, forward
        )
        high = lax.ppermute(lax.slice_in_dim(block, 0, width, axis=dim), axis, backward)
        block = jnp.concatenate([low, block, high], axis=dim)
    return block


def in_blocks(shard, dim, peers):
    dims = shard.shape
    tiles = shard.reshape(*dims[:dim], peers, dims[dim] // peers, *dims[dim + 1 :])
    return jnp.moveaxis(tiles, dim, 0)


def sum_at_owner(shard, axis, dim):
    tiles = in_blocks(shard, dim, lax.axis_size(axis))
    arrived = lax.all_to_all(tiles, axis, split_axis=0, concat_axis=0, tiled=True)
    return arrived.sum(axis=0)


def sum_by_axis(shard, axes, dim):
    far, near = axes
    own = sum_at_owner(in_blocks(shard, dim, lax.axis_size(far)), near, dim + 1)
    return jnp.sum(lax.all_to_all(own, far, 0, 0, tiled=True), axis=0)


def padded_to(lines, peers):
    spare = -lines.shape[0] % peers
    if not spare:
        return lines
    return jnp.concatenate([lines, jnp.zeros((spare, *lines.shape[1:]), lines.dtype)])


def sent_to_all(shard, axis):
    copies = jnp.broadcast_to(shard, (lax.axis_size(axis), *shard.shape))
    return lax.all_to_all(copies, axis, split_axis=0, concat_axis=0, tiled=True)


def joined_along(tiles, dim):
    dims = list(tiles.shape[1:])
    dims[dim] *= tiles.shape[0]
    return jnp.moveaxis(tiles, 0, dim).reshape(dims)


def whole_of(shard, axes, dim):
    far, near = axes
    tiles = sent_to_all(sent_to_all(shard, far), near)
    return joined_along(tiles.swapaxes(0, 1).reshape(-1, *shard.shape), dim)


def nested_sum(shard, axes):
    own = sum_by_axis(padded_to(shard, lax.axis_size(axes[0]) * lax.axis_size(axes[1])), axes, 0)
    whole = whole_of(own, axes, 0)
    return whole[: len(shard)].reshape(shard.shape)


def packed_total(arrays, axis):
    ends = [0]
    for a in arrays:
        ends.append(ends[-1] + a.size)
    so_far = nested_sum(jnp.concatenate([a.ravel() for a in arrays]), axis)
    return tuple((so_far[b:e].reshape(a.shape) for a, b, e in zip(arrays, ends, ends[1:])))


def gathered_copies(shard, axis, dim):
    return joined_along(sent_to_all(shard, axis), dim)


def total_of(shard, axes):
    lines = shard.reshape(-1)
    own = sum_by_axis(padded_to(lines, lax.axis_size(axes[0]) * lax.axis_size(axes[1])), axes, 0)
    whole = whole_of(own, axes, 0)
    return whole[: len(lines)].reshape(shard.shape)


def silu_slope(values):
    sigma = jax.nn.sigmoid(values)
    return sigma * (1.0 + values * (1.0 - sigma))


def edge_forward(extended, own_rows, sources, targets, w_send, w_recv, w_node):
    preact = jnp.dot(extended[sources], w_send, preferred_element_type=jnp.float32)
    preact = preact + jnp.dot(own_rows[targets], w_recv, preferred_element_type=jnp.float32)
    message = jax.nn.silu(preact).astype(jnp.bfloat16)
    summed = jax.ops.segment_sum(
        message.astype(jnp.float32), targets, num_segments=own_rows.shape[0]
    ).astype(jnp.bfloat16)
    updated = (
        own_rows.astype(jnp.float32) + jnp.dot(summed, w_node, preferred_element_type=jnp.float32)
    ).astype(jnp.bfloat16)
    return (updated, preact)


def edge_backward(grad_out, extended, own_rows, preact, sources, targets, w_send, w_recv, w_node):
    rounded = grad_out.astype(jnp.bfloat16)
    grad_sum = jnp.dot(rounded, w_node.T, preferred_element_type=jnp.float32)
    grad_pre = (grad_sum[targets] * silu_slope(preact)).astype(jnp.bfloat16)
    grad_ext = jax.ops.segment_sum(
        jnp.dot(grad_pre, w_send.T, preferred_element_type=jnp.float32),
        sources,
        num_segments=extended.shape[0],
    )
    own_count = own_rows.shape[0]
    grad_own = grad_out + jax.ops.segment_sum(
        jnp.dot(grad_pre, w_recv.T, preferred_element_type=jnp.float32),
        targets,
        num_segments=own_count,
    )
    grad_own = grad_own + grad_ext[:own_count]
    grad_weight = lax.dot_general(
        extended[sources], grad_pre, (((0,), (0,)), ((), ())), preferred_element_type=jnp.float32
    )
    return (grad_own, grad_ext[own_count:], grad_weight)


def top_forward(pooled, w_top):
    slope_in = jnp.dot(pooled.astype(jnp.bfloat16), w_top, preferred_element_type=jnp.float32)
    return ((pooled + jax.nn.silu(slope_in)).astype(jnp.bfloat16), slope_in)


def top_backward(grad_top, slope_in, w_top):
    inner = (grad_top * silu_slope(slope_in)).astype(jnp.bfloat16)
    return grad_top + jnp.dot(inner, w_top.T, preferred_element_type=jnp.float32)


def add_rows(grads, index, values):
    padded = jnp.concatenate([grads, jnp.zeros((1, grads.shape[1]), jnp.float32)], axis=0)
    return padded.at[index].add(values)[:-1]


def local(
    features,
    cotangent,
    fine_send,
    fine_rim,
    fine_src,
    fine_dst,
    fine_pool,
    coarse_send,
    coarse_src,
    coarse_dst,
    coarse_pool,
    w_send,
    w_recv,
    w_node,
    v_send,
    v_recv,
    v_node,
    w_top,
):
    width = features.shape[1]
    dom_count = lax.axis_size(DOM)
    coarse_count = coarse_pool.shape[0]
    group_coarse = coarse_count * dom_count
    slot_rows = fine_send.shape[1]
    coarse_slots = coarse_send.shape[1]
    rim_count = fine_rim.shape[1]
    padded = jnp.concatenate([features, jnp.zeros((1, width), jnp.bfloat16)], axis=0)
    incoming = lax.all_to_all(
        padded[fine_send], DOM, split_axis=0, concat_axis=0, tiled=True
    ).reshape(-1, width)
    rim_rows = with_halo(features[fine_rim], (("group", 0),), 1)
    extended = jnp.concatenate([features, incoming, rim_rows[0], rim_rows[3]], axis=0)
    updated, preact = edge_forward(extended, features, fine_src, fine_dst, w_send, w_recv, w_node)
    partial_value = jax.ops.segment_sum(
        updated.astype(jnp.float32), fine_pool, num_segments=group_coarse
    )
    grad_flow = cotangent.astype(jnp.float32)
    grad_partial = jax.ops.segment_sum(grad_flow, fine_pool, num_segments=group_coarse)
    owned = sum_at_owner(partial_value, DOM, 0)
    grad_coarse = sum_at_owner(grad_partial, DOM, 0)
    coarse_in = (0.25 * owned).astype(jnp.bfloat16)
    cpadded = jnp.concatenate([coarse_in, jnp.zeros((1, width), jnp.bfloat16)], axis=0)
    cincoming = lax.all_to_all(
        cpadded[coarse_send], DOM, split_axis=0, concat_axis=0, tiled=True
    ).reshape(-1, width)
    cextended = jnp.concatenate([coarse_in, cincoming], axis=0)
    coarse_mid, cpreact = edge_forward(
        cextended, coarse_in, coarse_src, coarse_dst, v_send, v_recv, v_node
    )
    top_partial = jax.ops.segment_sum(coarse_mid.astype(jnp.float32), coarse_pool, num_segments=NCC)
    grad_top_partial = jax.ops.segment_sum(grad_coarse, coarse_pool, num_segments=NCC)
    top_total, grad_top = packed_total(
        (top_partial, grad_top_partial), (("group", "dom_0"), ("dom_1", "dom_2"))
    )
    pooled = 0.125 * top_total
    top_out, slope_in = top_forward(pooled, w_top)
    coarse_out = (coarse_mid.astype(jnp.float32) + top_out[coarse_pool].astype(jnp.float32)).astype(
        jnp.bfloat16
    )
    coarse_table = gathered_copies(coarse_out, DOM, 0)
    flow = (updated.astype(jnp.float32) + coarse_table[fine_pool].astype(jnp.float32)).astype(
        jnp.bfloat16
    )
    grad_pool = top_backward(grad_top, slope_in, w_top)
    grad_cmid = grad_coarse + 0.125 * grad_pool[coarse_pool]
    c_own, c_halo, c_weight = edge_backward(
        grad_cmid, cextended, coarse_in, cpreact, coarse_src, coarse_dst, v_send, v_recv, v_node
    )
    creturned = lax.all_to_all(
        c_halo.reshape(dom_count, coarse_slots, width), DOM, split_axis=0, concat_axis=0, tiled=True
    )
    grad_cin = add_rows(c_own, coarse_send.reshape(-1), creturned.reshape(-1, width))
    grad_table = gathered_copies(grad_cin, DOM, 0)
    grad_fmid = grad_flow + 0.25 * grad_table[fine_pool]
    f_own, f_halo, f_weight = edge_backward(
        grad_fmid, extended, features, preact, fine_src, fine_dst, w_send, w_recv, w_node
    )
    split = dom_count * slot_rows
    returned = lax.all_to_all(
        f_halo[:split].reshape(dom_count, slot_rows, width),
        DOM,
        split_axis=0,
        concat_axis=0,
        tiled=True,
    )
    grad_x = add_rows(f_own, fine_send.reshape(-1), returned.reshape(-1, width))
    rim_grads = jnp.stack([f_halo[split : split + rim_count], f_halo[split + rim_count :]], axis=0)
    rim_back = with_halo(rim_grads, (("group", 0),), 1)
    rim_values = jnp.concatenate([rim_back[0], rim_back[3]], axis=0)
    grad_x = add_rows(grad_x, fine_rim.reshape(-1), rim_values)
    grad_send = total_of(f_weight, (("group", "dom_0"), ("dom_1", "dom_2")))
    return (flow, grad_x, grad_send)


def solution(mesh):
    torus = Mesh(
        mesh.devices.reshape(mesh.shape["group"], 4, 4, 2), ("group", "dom_0", "dom_1", "dom_2")
    )
    in_specs = (
        P(GROUP_DOM, None),
        P(GROUP_DOM, None),
        P(GROUP_DOM, None),
        P(GROUP_DOM, None),
        P(GROUP_DOM),
        P(GROUP_DOM),
        P(GROUP_DOM),
        P(GROUP_DOM, None),
        P(GROUP_DOM),
        P(GROUP_DOM),
        P(GROUP_DOM),
        P(),
        P(),
        P(),
        P(),
        P(),
        P(),
        P(),
    )
    out_specs = (P(GROUP_DOM, None), P(GROUP_DOM, None), P())
    return jax.shard_map(local, mesh=torus, in_specs=in_specs, out_specs=out_specs, check_vma=False)
```

profile of v0, /device:TPU:1, one launch (start us, length us, event | category | flops | bytes accessed | tf_op | source)
XLA Modules:
  0.0 359.4 jit_solution(9927327569319083981)
XLA Ops:
  4.4 5.0 %collective-permute-start = (bf16[1,128,128]{2,1,0:T(8,128)(2,1)S(1)}, bf16[1,128,128]{2,1,0:T(8,128)(2,1)S(1)}, u32[]{:S(2)}, u32[]{:S(2)}) collective-permute-start(bf16[1,128,128]{2,1,0:T(8,128)(2,1)S(1)} %get-tuple-element.9), channel_id=1, source_target_pairs={{0,32},{32,64},{64,96},{96,128},{128,160},{160,192},{192,224},{1,3... | collective-permute-start | bytes 98312 | tf_op jit(solution)/shard_map/ppermute | solution.py:17
  13.1 8.1 %all-to-all-start = ((bf16[32,16,128]{2,1,0:T(8,128)(2,1)}), bf16[32,16,128]{2,1,0:T(8,128)(2,1)S(1)}, u32[]{:S(2)}, u32[]{:S(2)}) async-start(bf16[32,16,128]{2,1,0:T(8,128)(2,1)} %bitcast), calls=%async_computation | async-start | bytes 262144 | tf_op jit(solution)/shard_map/all_to_all | solution.py:175
  21.3 12.1 %gather_fusion.3 = bf16[4096,128]{1,0:T(8,128)(2,1)S(1)} fusion(bf16[512,128]{1,0:T(8,128)(2,1)S(1)} %copy-done.1, s32[4096]{0:T(1024)S(1)} %fusion.39), kind=kCustom, calls=%fused_computation.3 | custom fusion | bytes 2113536 | tf_op jit(solution)/shard_map/gather | solution.py:99
  35.2 12.1 %gather_fusion.2 = bf16[4096,128]{1,0:T(8,128)(2,1)S(1)} fusion(bf16[1280,128]{1,0:T(8,128)(2,1)S(1)} %pad_maximum_fusion, s32[4096]{0:T(1024)S(1)} %fusion.38), kind=kCustom, calls=%fused_computation.2 | custom fusion | bytes 2113536 | tf_op jit(solution)/shard_map/gather | solution.py:98
  49.9 23.5 %scatter_custom_fusion = f32[512,128]{1,0:T(8,128)} fusion(s32[4096]{0:T(1024)S(1)} %copy-done.19, f32[4096,128]{1,0:T(8,128)S(1)} %convolution_add_fusion, f32[]{:T(128)} %constant.20.clone.1, f32[]{:T(128)} %constant.14.clone.1), kind=kCustom, calls=%fused_computation.28 | custom fusion | flops 3670016 | bytes 2359304 | tf_op jit(solution)/shard_map/scatter-add | solution.py:101
  77.7 7.4 %all-to-all-start.1 = ((f32[32,32,128]{2,1,0:T(8,128)}), f32[32,32,128]{2,1,0:T(8,128)S(1)}, u32[]{:S(2)}, u32[]{:S(2)}) async-start(f32[32,32,128]{2,1,0:T(8,128)} %bitcast.7), calls=%async_computation.1 | async-start | bytes 1048576 | tf_op jit(solution)/shard_map/all_to_all | solution.py:33
  88.5 8.0 %all-to-all-done.1 = f32[32,32,128]{2,1,0:T(8,128)S(1)} async-done(((f32[32,32,128]{2,1,0:T(8,128)}), f32[32,32,128]{2,1,0:T(8,128)S(1)}, u32[]{:S(2)}, u32[]{:S(2)}) %all-to-all-start.1) | async-done | bytes 524320 | tf_op jit(solution)/shard_map/all_to_all | solution.py:33
  102.0 10.1 %all-to-all-done.3 = f32[32,32,128]{2,1,0:T(8,128)S(1)} async-done(((f32[32,32,128]{2,1,0:T(8,128)}), f32[32,32,128]{2,1,0:T(8,128)S(1)}, u32[]{:S(2)}, u32[]{:S(2)}) %all-to-all-start.3) | async-done | bytes 524320 | tf_op jit(solution)/shard_map/all_to_all | solution.py:33
  117.9 5.5 %all-to-all-done.2 = bf16[32,4,128]{2,1,0:T(4,128)(2,1)S(1)} async-done(((bf16[32,4,128]{2,1,0:T(4,128)(2,1)}), bf16[32,4,128]{2,1,0:T(4,128)(2,1)S(1)}, u32[]{:S(2)}, u32[]{:S(2)}) %all-to-all-start.2) | async-done | bytes 32800 | tf_op jit(solution)/shard_map/all_to_all | solution.py:190
  128.5 12.2 %all_to_all.96 = f32[8,32,512]{2,1,0:T(8,128)S(1)} all-to-all(f32[8,32,512]{2,1,0:T(8,128)S(1)} %copy.45), channel_id=1, replica_groups=mesh['group'=8,'dom_0'=4,'dom_1'=4,'dom_2'=2] {'dom_1','dom_2'}, dimensions={0} | all-to-all | bytes 1048576 | tf_op jit(solution)/shard_map/all_to_all | solution.py:33
  140.8 17.9 %all_to_all.97 = f32[32,1,512]{2,1,0:T(1,128)S(1)} all-to-all(f32[32,1,512]{2,1,0:T(1,128)S(1)} %all_to_all.65), channel_id=1, replica_groups=mesh['group'=8,'dom_0'=4,'dom_1'=4,'dom_2'=2] {'group','dom_0'}, dimensions={0} | all-to-all | bytes 131072 | tf_op jit(solution)/shard_map/all_to_all | solution.py:40
  163.3 8.9 %all-to-all-done.6 = f32[32,1,512]{2,1,0:T(1,128)S(1)} async-done(((f32[32,1,512]{2,1,0:T(1,128)}), f32[32,1,512]{2,1,0:T(1,128)S(1)}, u32[]{:S(2)}, u32[]{:S(2)}) %all-to-all-start.6) | async-done | bytes 65568 | tf_op jit(solution)/shard_map/all_to_all | solution.py:52
  173.1 7.1 %all-to-all-start.7 = ((f32[8,32,512]{2,1,0:T(8,128)}), f32[8,32,512]{2,1,0:T(8,128)S(1)}, u32[]{:S(2)}, u32[]{:S(2)}) async-start(f32[8,32,512]{2,1,0:T(8,128)} %broadcast_in_dim.93), calls=%async_computation.7 | async-start | bytes 1048576 | tf_op jit(solution)/shard_map/all_to_all | solution.py:52
  182.2 7.3 %all-to-all-done.7 = f32[8,32,512]{2,1,0:T(8,128)S(1)} async-done(((f32[8,32,512]{2,1,0:T(8,128)}), f32[8,32,512]{2,1,0:T(8,128)S(1)}, u32[]{:S(2)}, u32[]{:S(2)}) %all-to-all-start.7) | async-done | bytes 524320 | tf_op jit(solution)/shard_map/all_to_all | solution.py:52
  201.7 5.4 %all-to-all-done.9 = f32[32,4,128]{2,1,0:T(4,128)S(1)} async-done(((f32[32,4,128]{2,1,0:T(4,128)}), f32[32,4,128]{2,1,0:T(4,128)S(1)}, u32[]{:S(2)}, u32[]{:S(2)}) %all-to-all-start.9) | async-done | bytes 65568 | tf_op jit(solution)/shard_map/all_to_all | solution.py:216
  214.7 10.2 %all-to-all-done.10 = f32[32,32,128]{2,1,0:T(8,128)S(1)} async-done(((f32[32,32,128]{2,1,0:T(8,128)}), f32[32,32,128]{2,1,0:T(8,128)S(1)}, u32[]{:S(2)}, u32[]{:S(2)}) %all-to-all-start.10) | async-done | bytes 524320 | tf_op jit(solution)/shard_map/all_to_all | solution.py:52
  232.0 14.2 %gather_fusion.12 = f32[4096,128]{1,0:T(8,128)} fusion(f32[512,128]{1,0:T(8,128)S(1)} %fusion.18, s32[4096]{0:T(1024)S(1)} %fusion.39), kind=kCustom, calls=%fused_computation.12 | custom fusion | bytes 4210688 | tf_op jit(solution)/shard_map/gather | solution.py:113
  250.1 4.8 %all-to-all-start.12 = ((f32[8,1,2048]{2,1,0:T(1,128)}), f32[8,1,2048]{2,1,0:T(1,128)S(1)}, u32[]{:S(2)}, u32[]{:S(2)}) async-start(f32[8,1,2048]{2,1,0:T(1,128)} %reshape.425), calls=%async_computation.12 | async-start | bytes 131072 | tf_op jit(solution)/shard_map/all_to_all | solution.py:33
  261.9 4.9 %all-to-all-start.13 = ((f32[32,1,64]{2,1,0:T(1,128)}), f32[32,1,64]{2,1,0:T(1,128)S(1)}, u32[]{:S(2)}, u32[]{:S(2)}) async-start(f32[32,1,64]{2,1,0:T(1,128)} %bitcast.28), calls=%async_computation.13 | async-start | bytes 32768 | tf_op jit(solution)/shard_map/all_to_all | solution.py:40
  267.4 7.8 %all-to-all-done.13 = f32[32,1,64]{2,1,0:T(1,128)S(1)} async-done(((f32[32,1,64]{2,1,0:T(1,128)}), f32[32,1,64]{2,1,0:T(1,128)S(1)}, u32[]{:S(2)}, u32[]{:S(2)}) %all-to-all-start.13) | async-done | bytes 8224 | tf_op jit(solution)/shard_map/all_to_all | solution.py:40
  281.8 22.8 %scatter_custom_fusion.9 = f32[1280,128]{1,0:T(8,128)S(1)} fusion(s32[4096]{0:T(1024)} %param.22, f32[4096,128]{1,0:T(8,128)} %fusion.55, f32[]{:T(128)} %constant.14.clone.1), kind=kCustom, calls=%fused_computation.45 | custom fusion | flops 524288 | bytes 655872 | tf_op jit(solution)/shard_map/scatter-add | solution.py:114
  305.5 5.5 %all-to-all-start.15 = ((f32[8,1,2048]{2,1,0:T(1,128)}), f32[8,1,2048]{2,1,0:T(1,128)S(1)}, u32[]{:S(2)}, u32[]{:S(2)}) async-start(f32[8,1,2048]{2,1,0:T(1,128)} %reshape.427), calls=%async_computation.15 | async-start | bytes 131072 | tf_op jit(solution)/shard_map/all_to_all | solution.py:52
  315.8 5.8 %all-to-all-start.11 = ((f32[32,16,128]{2,1,0:T(8,128)}), f32[32,16,128]{2,1,0:T(8,128)}, u32[]{:S(2)}, u32[]{:S(2)}) async-start(f32[32,16,128]{2,1,0:T(8,128)} %bitcast.19), calls=%async_computation.11 | async-start | bytes 524288 | tf_op jit(solution)/shard_map/all_to_all | solution.py:226
  322.1 22.5 %scatter_fusion.2 = f32[512,128]{1,0:T(8,128)S(1)} fusion(f32[512,128]{1,0:T(8,128)S(1)} %get-tuple-element.6, s32[4096]{0:T(1024)S(1)} %copy-done.19, f32[4096,128]{1,0:T(8,128)S(1)} %fusion.56), kind=kCustom, calls=%fused_computation.23 | custom fusion | flops 524288 | bytes 6307840 | tf_op jit(solution)/shard_map/scatter-add | solution.py:120
  (215 shorter events, 108.4 us)
Async XLA Ops:
  0.6 46.8 %copy-start = (bf16[128,128]{1,0:T(8,128)(2,1)S(1)}, bf16[128,128]{1,0:T(8,128)(2,1)}, u32[]{:S(2)}) copy-start(bf16[128,128]{1,0:T(8,128)(2,1)} %param.29) | copy-start | bytes 98308
  3.1 32.1 %collective-permute-start.1 = (bf16[1,128,128]{2,1,0:T(8,128)(2,1)S(1)}, bf16[1,128,128]{2,1,0:T(8,128)(2,1)S(1)}, u32[]{:S(2)}, u32[]{:S(2)}) collective-permute-start(bf16[1,128,128]{2,1,0:T(8,128)(2,1)S(1)} %get-tuple-element.10), channel_id=1, source_target_pairs={{32,0},{64,32},{96,64},{128,96},{160,128},{192,160},{224,192},{33,... | collective-permute-start | bytes 98312 | tf_op jit(solution)/shard_map/ppermute | solution.py:20
  4.4 30.8 %collective-permute-start = (bf16[1,128,128]{2,1,0:T(8,128)(2,1)S(1)}, bf16[1,128,128]{2,1,0:T(8,128)(2,1)S(1)}, u32[]{:S(2)}, u32[]{:S(2)}) collective-permute-start(bf16[1,128,128]{2,1,0:T(8,128)(2,1)S(1)} %get-tuple-element.9), channel_id=1, source_target_pairs={{0,32},{32,64},{64,96},{96,128},{128,160},{160,192},{192,224},{1,3... | collective-permute-start | bytes 98312 | tf_op jit(solution)/shard_map/ppermute | solution.py:17
  13.1 22.1 %all-to-all-start = ((bf16[32,16,128]{2,1,0:T(8,128)(2,1)}), bf16[32,16,128]{2,1,0:T(8,128)(2,1)S(1)}, u32[]{:S(2)}, u32[]{:S(2)}) async-start(bf16[32,16,128]{2,1,0:T(8,128)(2,1)} %bitcast), calls=%async_computation | async-start | bytes 262144 | tf_op jit(solution)/shard_map/all_to_all | solution.py:175
  49.8 35.5 %copy-start.7 = (bf16[512,128]{1,0:T(8,128)(2,1)S(1)}, bf16[512,128]{1,0:T(8,128)(2,1)}, u32[]{:S(2)}) copy-start(bf16[512,128]{1,0:T(8,128)(2,1)} %param.19) | copy-start | bytes 393220
  49.8 38.6 %copy-start.36 = (s32[256]{0:T(256)S(1)}, s32[256]{0:T(256)}, u32[]{:S(2)}) copy-start(s32[256]{0:T(256)} %param.26) | copy-start | bytes 3076
  77.7 18.8 %all-to-all-start.1 = ((f32[32,32,128]{2,1,0:T(8,128)}), f32[32,32,128]{2,1,0:T(8,128)S(1)}, u32[]{:S(2)}, u32[]{:S(2)}) async-start(f32[32,32,128]{2,1,0:T(8,128)} %bitcast.7), calls=%async_computation.1 | async-start | bytes 1048576 | tf_op jit(solution)/shard_map/all_to_all | solution.py:33
  96.5 15.6 %all-to-all-start.3 = ((f32[32,32,128]{2,1,0:T(8,128)}), f32[32,32,128]{2,1,0:T(8,128)S(1)}, u32[]{:S(2)}, u32[]{:S(2)}) async-start(f32[32,32,128]{2,1,0:T(8,128)} %bitcast.68), calls=%async_computation.3 | async-start | bytes 1048576 | tf_op jit(solution)/shard_map/all_to_all | solution.py:33
  112.1 11.3 %all-to-all-start.2 = ((bf16[32,4,128]{2,1,0:T(4,128)(2,1)}), bf16[32,4,128]{2,1,0:T(4,128)(2,1)S(1)}, u32[]{:S(2)}, u32[]{:S(2)}) async-start(bf16[32,4,128]{2,1,0:T(4,128)(2,1)} %bitcast.8), calls=%async_computation.2 | async-start | bytes 65536 | tf_op jit(solution)/shard_map/all_to_all | solution.py:190
  128.5 51.7 %copy-start.27 = (s32[32,4]{0,1:T(4,128)S(1)}, s32[32,4]{0,1:T(4,128)}, u32[]{:S(2)}) copy-start(s32[32,4]{0,1:T(4,128)} %param.25) | copy-start | bytes 1540
  128.5 51.8 %copy-start.20 = (s32[32,16]{0,1:T(8,128)S(1)}, s32[32,16]{0,1:T(8,128)}, u32[]{:S(2)}) copy-start(s32[32,16]{0,1:T(8,128)} %param.20) | copy-start | bytes 6148
  128.5 53.1 %copy-start.34 = (s32[512]{0:T(512)S(1)}, s32[512]{0:T(512)}, u32[]{:S(2)}) copy-start(s32[512]{0:T(512)} %param.24) | copy-start | bytes 6148
  159.5 12.7 %all-to-all-start.6 = ((f32[32,1,512]{2,1,0:T(1,128)}), f32[32,1,512]{2,1,0:T(1,128)S(1)}, u32[]{:S(2)}, u32[]{:S(2)}) async-start(f32[32,1,512]{2,1,0:T(1,128)} %broadcast_in_dim.92), calls=%async_computation.6 | async-start | bytes 131072 | tf_op jit(solution)/shard_map/all_to_all | solution.py:52
  173.1 16.5 %all-to-all-start.7 = ((f32[8,32,512]{2,1,0:T(8,128)}), f32[8,32,512]{2,1,0:T(8,128)S(1)}, u32[]{:S(2)}, u32[]{:S(2)}) async-start(f32[8,32,512]{2,1,0:T(8,128)} %broadcast_in_dim.93), calls=%async_computation.7 | async-start | bytes 1048576 | tf_op jit(solution)/shard_map/all_to_all | solution.py:52
  195.2 11.9 %all-to-all-start.9 = ((f32[32,4,128]{2,1,0:T(4,128)}), f32[32,4,128]{2,1,0:T(4,128)S(1)}, u32[]{:S(2)}, u32[]{:S(2)}) async-start(f32[32,4,128]{2,1,0:T(4,128)} %bitcast.15), calls=%async_computation.9 | async-start | bytes 131072 | tf_op jit(solution)/shard_map/all_to_all | solution.py:216
  209.2 15.6 %all-to-all-start.10 = ((f32[32,32,128]{2,1,0:T(8,128)}), f32[32,32,128]{2,1,0:T(8,128)S(1)}, u32[]{:S(2)}, u32[]{:S(2)}) async-start(f32[32,32,128]{2,1,0:T(8,128)} %broadcast_in_dim.99), calls=%async_computation.10 | async-start | bytes 1048576 | tf_op jit(solution)/shard_map/all_to_all | solution.py:52
  225.6 24.4 %all-to-all-start.8 = ((bf16[32,32,128]{2,1,0:T(8,128)(2,1)}), bf16[32,32,128]{2,1,0:T(8,128)(2,1)}, u32[]{:S(2)}, u32[]{:S(2)}) async-start(bf16[32,32,128]{2,1,0:T(8,128)(2,1)} %broadcast_in_dim.95), calls=%async_computation.8 | async-start | bytes 524288 | tf_op jit(solution)/shard_map/all_to_all | solution.py:52
  250.1 9.7 %all-to-all-start.12 = ((f32[8,1,2048]{2,1,0:T(1,128)}), f32[8,1,2048]{2,1,0:T(1,128)S(1)}, u32[]{:S(2)}, u32[]{:S(2)}) async-start(f32[8,1,2048]{2,1,0:T(1,128)} %reshape.425), calls=%async_computation.12 | async-start | bytes 131072 | tf_op jit(solution)/shard_map/all_to_all | solution.py:33
  261.9 13.4 %all-to-all-start.13 = ((f32[32,1,64]{2,1,0:T(1,128)}), f32[32,1,64]{2,1,0:T(1,128)S(1)}, u32[]{:S(2)}, u32[]{:S(2)}) async-start(f32[32,1,64]{2,1,0:T(1,128)} %bitcast.28), calls=%async_computation.13 | async-start | bytes 32768 | tf_op jit(solution)/shard_map/all_to_all | solution.py:40
  276.0 28.7 %all-to-all-start.14 = ((f32[32,1,64]{2,1,0:T(1,128)}), f32[32,1,64]{2,1,0:T(1,128)S(1)}, u32[]{:S(2)}, u32[]{:S(2)}) async-start(f32[32,1,64]{2,1,0:T(1,128)} %broadcast_in_dim.102), calls=%async_computation.14 | async-start | bytes 32768 | tf_op jit(solution)/shard_map/all_to_all | solution.py:52
  305.5 10.3 %all-to-all-start.15 = ((f32[8,1,2048]{2,1,0:T(1,128)}), f32[8,1,2048]{2,1,0:T(1,128)S(1)}, u32[]{:S(2)}, u32[]{:S(2)}) async-start(f32[8,1,2048]{2,1,0:T(1,128)} %reshape.427), calls=%async_computation.15 | async-start | bytes 131072 | tf_op jit(solution)/shard_map/all_to_all | solution.py:52
  315.8 36.7 %all-to-all-start.11 = ((f32[32,16,128]{2,1,0:T(8,128)}), f32[32,16,128]{2,1,0:T(8,128)}, u32[]{:S(2)}, u32[]{:S(2)}) async-start(f32[32,16,128]{2,1,0:T(8,128)} %bitcast.19), calls=%async_computation.11 | async-start | bytes 524288 | tf_op jit(solution)/shard_map/all_to_all | solution.py:226
  345.5 11.0 %collective-permute-start.3 = (f32[1,128,128]{2,1,0:T(8,128)S(1)}, f32[1,128,128]{2,1,0:T(8,128)S(1)}, u32[]{:S(2)}, u32[]{:S(2)}) collective-permute-start(f32[1,128,128]{2,1,0:T(8,128)S(1)} %get-tuple-element.4), channel_id=1, source_target_pairs={{32,0},{64,32},{96,64},{128,96},{160,128},{192,160},{224,192},{33,... | collective-permute-start | bytes 196616 | tf_op jit(solution)/shard_map/ppermute | solution.py:20
  346.8 9.7 %collective-permute-start.2 = (f32[1,128,128]{2,1,0:T(8,128)S(1)}, f32[1,128,128]{2,1,0:T(8,128)S(1)}, u32[]{:S(2)}, u32[]{:S(2)}) collective-permute-start(f32[1,128,128]{2,1,0:T(8,128)S(1)} %get-tuple-element.3), channel_id=1, source_target_pairs={{0,32},{32,64},{64,96},{96,128},{128,160},{160,192},{192,224},{1,3... | collective-permute-start | bytes 196616 | tf_op jit(solution)/shard_map/ppermute | solution.py:17
  (34 other events, 555.6 us)
where the time goes:
time: 361 us; the launch traced here: 359 us
  other arithmetic  99.8 us (28%)
  starting transfers between devices  84.1 us (23%)
  waiting for transfers between devices  69.6 us (19%)
  local copies, waits for them, and re-layouts  63.1 us (17%)
  blocking collectives  30.1 us (8%)
  matrix products  10.9 us (3%)
    all_to_all x6, waiting for transfers between devices, sent_to_all(): return lax.all_to_all(copies, axis, split_axis=0, concat_axis=0, tiled=True)  30.5 us
    all_to_all x6, starting transfers between devices, sent_to_all(): return lax.all_to_all(copies, axis, split_axis=0, concat_axis=0, tiled=True)  29.1 us
    scatter-add x2, other arithmetic, edge_forward(): jax.ops.segment_sum(message.astype(jnp.float32), targets, num_segments=ow...  25.2 us
    scatter-add x2, other arithmetic, edge_backward(): jax.ops.segment_sum(jnp.dot(grad_pre, w_recv.T, preferred_element_type=jn...  24.4 us
    scatter-add x2, other arithmetic, edge_backward(): jax.ops.segment_sum(jnp.dot(grad_pre, w_send.T, preferred_element_type=jn...  24.4 us
    all_to_all x3, waiting for transfers between devices, sum_at_owner(): lax.all_to_all(tiles, axis, split_axis=0, concat_axis=0, tiled=True)  20.3 us
    all_to_all x1, blocking collectives, sum_by_axis(): return jnp.sum(lax.all_to_all(own, far, 0, 0, tiled=True), axis=0)  17.9 us
    all_to_all x3, starting transfers between devices, sum_at_owner(): lax.all_to_all(tiles, axis, split_axis=0, concat_axis=0, tiled=True)  16.3 us
  transfers between devices with their start and end apart: 18, of which 10 were waited for; matrix products, arithmetic and copies ran while one was open for 30% of the time, Pallas kernels for 0%

commit v1 on v0

v1 whole, which is shorter than its diff:
```python
import functools

import jax
import jax.numpy as jnp
from jax import lax
from jax.experimental import pallas as pl
from jax.experimental.pallas import tpu as pltpu
from jax.sharding import PartitionSpec as P

F32 = jnp.float32
BF16 = jnp.bfloat16
MESH = pl.DeviceIdType.MESH

H = 128
NODE = 512
EDGE = 4096
SLOT = 16
RIM = 128
NC = 32
CEDGE = 256
CSLOT = 4
NCC = 512
BLK = 1024

R_SRC, R_DST, R_POOL, R_SEND, R_CSEND, R_CSRC, R_CDST, R_CPOOL = 0, 32, 64, 68, 74, 78, 80, 82
R_ALL = 88


def nn(a, b):
    return jnp.dot(a, b, preferred_element_type=F32)


def nt(a, b):
    return lax.dot_general(a, b, (((1,), (1,)), ((), ())), preferred_element_type=F32)


def tn(a, b):
    return lax.dot_general(a, b, (((0,), (0,)), ((), ())), preferred_element_type=F32)


def hot_rows(count, row, base=0):
    at = lax.broadcasted_iota(jnp.int32, (count, 128), 0) + base
    return jnp.where(at == row, 1.0, 0.0).astype(BF16)


def hot_cols(count, row):
    idx = jnp.transpose(jnp.broadcast_to(row, (128, 128)))
    parts = []
    for m in range(count // 128):
        at = lax.broadcasted_iota(jnp.int32, (128, 128), 1) + 128 * m
        parts.append(jnp.where(at == idx, 1.0, 0.0).astype(BF16))
    return jnp.concatenate(parts, axis=1) if len(parts) > 1 else parts[0]


def gate(v):
    return 0.5 + 0.5 * jnp.tanh(0.5 * v)


def kernel(
    ng, nd,
    feat, cot, idx, w_send, w_recv, w_node, v_send, v_recv, v_node, w_top,
    flow, grad_x, grad_w,
    oht, ohp, ohpr, ohs, ohc, slope, sacc,
    ext, zt, out_a, gsend, gbuf, psend, pbuf, csend, cext, tsend, tbuf, hsend2, hbuf2,
    zsend, zbuf, zsend2, zbuf2, tout, ttab, eout, etab, fsend, fbuf, gout, gtab,
    hsend, hbuf, wsend, wbuf, wmid, wbuf2, wout, wtab,
    ssem, rsem,
):
    g = lax.axis_index("group")
    d = lax.axis_index("dom")

    barrier = pltpu.get_barrier_semaphore()

    def greet_dom(j, c):
        pl.semaphore_signal(barrier, inc=1, device_id=(g, lax.rem(d + j, nd)), device_id_type=MESH)
        return c

    def greet_group(j, c):
        pl.semaphore_signal(barrier, inc=1, device_id=(lax.rem(g + j, ng), d), device_id_type=MESH)
        return c

    lax.fori_loop(1, nd, greet_dom, 0)
    lax.fori_loop(1, ng, greet_group, 0)

    def to_dom(ph, src, dst):
        def step(j, c):
            p = lax.rem(d + j, nd)
            pltpu.make_async_remote_copy(
                src_ref=src(p), dst_ref=dst, send_sem=ssem.at[ph], recv_sem=rsem.at[ph],
                device_id=(g, p), device_id_type=MESH,
            ).start()
            return c

        lax.fori_loop(1, nd, step, 0)

    def to_group(ph, src, dst):
        def step(j, c):
            q = lax.rem(g + j, ng)
            pltpu.make_async_remote_copy(
                src_ref=src(q), dst_ref=dst, send_sem=ssem.at[ph], recv_sem=rsem.at[ph],
                device_id=(q, d), device_id_type=MESH,
            ).start()
            return c

        lax.fori_loop(1, ng, step, 0)

    def to_one(ph, src, dst, q):
        pltpu.make_async_remote_copy(
            src_ref=src, dst_ref=dst, send_sem=ssem.at[ph], recv_sem=rsem.at[ph],
            device_id=(q, d), device_id_type=MESH,
        ).start()

    waits = []

    def arrived(ph, ref):
        pltpu.make_async_copy(ref, ref, rsem.at[ph]).wait()
        waits.append((ph, ref))

    def rows(ref, at, count):
        return ref.at[pl.ds(pl.multiple_of(at, 8), count)]

    ext[0:NODE, :] = feat[...]
    x = feat[...]
    for k in range(6):
        row = idx[R_SEND + k : R_SEND + k + 1, :]
        ohs[:, 128 * k : 128 * k + 128] = hot_rows(NODE, row)
        out_a[128 * k : 128 * k + 128, :] = nn(hot_cols(NODE, row), x).astype(BF16)

    pl.semaphore_wait(barrier, nd - 1 + ng - 1)
    nslot = nd * SLOT
    prev, nxt = lax.rem(g + ng - 1, ng), lax.rem(g + 1, ng)
    to_one(1, out_a.at[nslot : nslot + RIM], ext.at[NODE + nslot + RIM : NODE + nslot + 2 * RIM], prev)
    to_one(1, out_a.at[nslot + RIM : nslot + 2 * RIM], ext.at[NODE + nslot : NODE + nslot + RIM], nxt)
    to_dom(0, lambda p: rows(out_a, p * SLOT, SLOT), rows(ext, NODE + d * SLOT, SLOT))
    rows(ext, NODE + d * SLOT, SLOT)[...] = rows(out_a, d * SLOT, SLOT)[...]

    for k in range(4):
        row = idx[R_POOL + k : R_POOL + k + 1, :]
        ohp[:, 128 * k : 128 * k + 128] = hot_rows(nd * NC, row)
        ohpr[128 * k : 128 * k + 128, :] = hot_cols(nd * NC, row)
    gsend[...] = nn(ohp[...], cot[...]).astype(BF16)
    to_dom(2, lambda p: rows(gsend, p * NC, NC), gbuf.at[d])
    gbuf[d] = rows(gsend, d * NC, NC)[...]

    next_rows = NODE + nslot + 2 * RIM

    def build(b, c):
        for r in range(BLK // 128):
            src = idx[pl.ds(R_SRC + b * (BLK // 128) + r, 1), :]
            dst = idx[pl.ds(R_DST + b * (BLK // 128) + r, 1), :]
            oht[b, 0:next_rows, 128 * r : 128 * r + 128] = hot_rows(next_rows, src)
            oht[b, next_rows : next_rows + NODE, 128 * r : 128 * r + 128] = hot_rows(NODE, dst)
        return c

    lax.fori_loop(0, EDGE // BLK, build, 0)

    c_rows = NC + nd * SLOT
    for k in range(CEDGE // 128):
        src = idx[R_CSRC + k : R_CSRC + k + 1, :]
        dst = idx[R_CDST + k : R_CDST + k + 1, :]
        ohc[0:c_rows, 128 * k : 128 * k + 128] = hot_rows(c_rows, src)
        ohc[c_rows : c_rows + NC, 128 * k : 128 * k + 128] = hot_rows(NC, dst)
    cpool = idx[R_CPOOL : R_CPOOL + 1, :]

    ws_t = jnp.transpose(w_send[...].astype(F32)).astype(BF16)
    wr_t = jnp.transpose(w_recv[...].astype(F32)).astype(BF16)
    vs_t = jnp.transpose(v_send[...].astype(F32)).astype(BF16)
    vr_t = jnp.transpose(v_recv[...].astype(F32)).astype(BF16)
    zt[:, 0:NODE] = nt(ws_t, x).astype(BF16)
    zt[:, next_rows : next_rows + NODE] = nt(wr_t, x).astype(BF16)

    arrived(0, ext.at[0 : (nd - 1) * SLOT])
    arrived(1, ext.at[0 : 2 * RIM])
    at = NODE + nslot
    ext[at : at + RIM, :] = jnp.where(g > 0, ext[at : at + RIM, :].astype(F32), 0.0).astype(BF16)
    ext[at + RIM : at + 2 * RIM, :] = jnp.where(
        g < ng - 1, ext[at + RIM : at + 2 * RIM, :].astype(F32), 0.0
    ).astype(BF16)
    zt[:, NODE:next_rows] = nt(ws_t, ext[NODE:next_rows, :]).astype(BF16)

    def forward(b, total):
        pre = nn(zt[...], oht[b])
        s = gate(pre)
        slope[b] = s * (1.0 + pre * (1.0 - s))
        msg = (pre * s).astype(BF16)
        return total + nt(oht[b, next_rows : next_rows + NODE, :], msg)

    summed = lax.fori_loop(0, EDGE // BLK, forward, jnp.zeros((NODE, H), F32))
    updated = (x.astype(F32) + nn(summed.astype(BF16), w_node[...])).astype(BF16)
    psend[...] = nn(ohp[...], updated).astype(BF16)
    to_dom(3, lambda p: rows(psend, p * NC, NC), pbuf.at[d])
    pbuf[d] = rows(psend, d * NC, NC)[...]

    ohtop = hot_rows(NCC, cpool)[:, 0:NC]
    tb = NCC // nd
    arrived(2, gbuf.at[0 : nd - 1])
    grad_coarse = jnp.sum(gbuf[...].astype(F32), axis=0)
    hsend2[...] = nn(ohtop, grad_coarse.astype(BF16)).astype(BF16)
    to_dom(4, lambda p: rows(hsend2, p * tb, tb), hbuf2.at[d])
    hbuf2[d] = rows(hsend2, d * tb, tb)[...]

    arrived(3, pbuf.at[0 : nd - 1])
    coarse_in = (0.25 * jnp.sum(pbuf[...].astype(F32), axis=0)).astype(BF16)
    ohcs = []
    for k in range(nd * SLOT // 128):
        row = idx[R_CSEND + k : R_CSEND + k + 1, :]
        csend[128 * k : 128 * k + 128, :] = nn(hot_cols(128, row)[:, 0:NC], coarse_in).astype(BF16)
        ohcs.append(hot_rows(NC, row))
    to_dom(5, lambda p: rows(csend, p * SLOT, SLOT), rows(cext, NC + d * SLOT, SLOT))
    cext[0:NC, :] = coarse_in
    rows(cext, NC + d * SLOT, SLOT)[...] = rows(csend, d * SLOT, SLOT)[...]

    arrived(4, hbuf2.at[0 : nd - 1])
    zsend2[...] = jnp.sum(hbuf2[...].astype(F32), axis=0)
    to_group(6, lambda q: zsend2, zbuf2.at[g])
    zbuf2[g] = zsend2[...]

    arrived(5, cext.at[0 : (nd - 1) * SLOT])
    cz = jnp.concatenate(
        [nt(vs_t, cext[...]).astype(BF16), nt(vr_t, coarse_in).astype(BF16)], axis=1
    )
    cpre = nn(cz, ohc[...])
    cs = gate(cpre)
    cslope = cs * (1.0 + cpre * (1.0 - cs))
    csum = nt(ohc[c_rows : c_rows + NC, :], (cpre * cs).astype(BF16))
    coarse_mid = (coarse_in.astype(F32) + nn(csum.astype(BF16), v_node[...])).astype(BF16)
    tsend[...] = nn(ohtop, coarse_mid).astype(BF16)
    to_dom(7, lambda p: rows(tsend, p * tb, tb), tbuf.at[d])
    tbuf[d] = rows(tsend, d * tb, tb)[...]

    arrived(6, zbuf2.at[0 : ng - 1])
    grad_top = jnp.sum(zbuf2[...], axis=0)

    arrived(7, tbuf.at[0 : nd - 1])
    zsend[...] = jnp.sum(tbuf[...].astype(F32), axis=0)
    to_group(8, lambda q: zsend, zbuf.at[g])
    zbuf[g] = zsend[...]
    arrived(8, zbuf.at[0 : ng - 1])
    pooled = 0.125 * jnp.sum(zbuf[...], axis=0)
    slope_in = nn(pooled.astype(BF16), w_top[...])
    ts = gate(slope_in)
    tout[0:tb, :] = (pooled + slope_in * ts).astype(BF16)
    inner = (grad_top * (ts * (1.0 + slope_in * (1.0 - ts)))).astype(BF16)
    tout[tb : 2 * tb, :] = (grad_top + nt(inner, w_top[...])).astype(BF16)
    to_dom(9, lambda p: tout, rows(ttab, d * 2 * tb, 2 * tb))
    rows(ttab, d * 2 * tb, 2 * tb)[...] = tout[...]

    lane = lax.broadcasted_iota(jnp.int32, (1, 128), 1)
    spot = (cpool // tb) * (2 * tb) + lax.rem(cpool, tb) + jnp.where(lane >= NC, tb, 0)
    picker = hot_cols(2 * NCC, jnp.where(lane < 2 * NC, spot, -1))
    arrived(9, ttab.at[0 : (nd - 1) * 2 * tb])
    picked = nn(picker, ttab[...])
    coarse_out = coarse_mid.astype(F32) + picked[0:NC, :]
    eout[...] = coarse_out.astype(BF16)
    to_dom(10, lambda p: eout, rows(etab, d * NC, NC))
    rows(etab, d * NC, NC)[...] = eout[...]

    grad_cmid = grad_coarse + 0.125 * picked[NC : 2 * NC, :]
    cgs = nt(v_node[...], grad_cmid.astype(BF16)).astype(BF16)
    cgp = (nn(cgs, ohc[c_rows : c_rows + NC, :]) * cslope).astype(BF16)
    csc = nt(ohc[...], cgp).astype(BF16)
    cge = nt(csc[0:c_rows, :], v_send[...])
    fsend[...] = cge[NC:c_rows, :].astype(BF16)
    to_dom(11, lambda p: rows(fsend, p * SLOT, SLOT), rows(fbuf, d * SLOT, SLOT))
    rows(fbuf, d * SLOT, SLOT)[...] = rows(fsend, d * SLOT, SLOT)[...]
    c_own = grad_cmid + nt(csc[c_rows : c_rows + NC, :], v_recv[...]) + cge[0:NC, :]
    ohcs = jnp.concatenate(ohcs, axis=1)
    arrived(11, fbuf.at[0 : (nd - 1) * SLOT])
    gout[...] = (c_own + nn(ohcs, fbuf[...])).astype(BF16)
    to_dom(12, lambda p: gout, rows(gtab, d * NC, NC))
    rows(gtab, d * NC, NC)[...] = gout[...]

    arrived(10, etab.at[0 : (nd - 1) * NC])
    flow[...] = (updated.astype(F32) + nn(ohpr[...], etab[...])).astype(BF16)

    arrived(12, gtab.at[0 : (nd - 1) * NC])
    grad_mid = cot[...].astype(F32) + 0.25 * nn(ohpr[...], gtab[...])
    gs = nt(w_node[...], grad_mid.astype(BF16)).astype(BF16)
    sacc[...] = jnp.zeros_like(sacc)

    def backward(b, c):
        gp = (nn(gs, oht[b, next_rows : next_rows + NODE, :]) * slope[b]).astype(BF16)
        sacc[...] += nt(oht[b], gp)
        return c

    lax.fori_loop(0, EDGE // BLK, backward, 0)
    s_src = sacc[0:next_rows, :].astype(BF16)
    wb = H // ng
    wsend[...] = tn(ext[...], s_src)
    to_group(13, lambda q: rows(wsend, q * wb, wb), wbuf.at[g])
    wbuf[g] = rows(wsend, g * wb, wb)[...]

    gext = nt(s_src, w_send[...])
    hsend[...] = gext[NODE:, :].astype(BF16)
    to_one(15, hsend.at[nslot : nslot + RIM], hbuf.at[nslot + RIM : nslot + 2 * RIM], prev)
    to_one(15, hsend.at[nslot + RIM : nslot + 2 * RIM], hbuf.at[nslot : nslot + RIM], nxt)
    to_dom(14, lambda p: rows(hsend, p * SLOT, SLOT), rows(hbuf, d * SLOT, SLOT))
    rows(hbuf, d * SLOT, SLOT)[...] = rows(hsend, d * SLOT, SLOT)[...]
    s_dst = sacc[next_rows : next_rows + NODE, :].astype(BF16)
    grad_x[...] = grad_mid + nt(s_dst, w_recv[...]) + gext[0:NODE, :]

    arrived(13, wbuf.at[0 : ng - 1])
    wmid[...] = jnp.sum(wbuf[...], axis=0)
    to_dom(16, lambda p: wmid, wbuf2.at[d])
    wbuf2[d] = wmid[...]

    arrived(14, hbuf.at[0 : (nd - 1) * SLOT])
    arrived(15, hbuf.at[0 : 2 * RIM])
    hbuf[nslot : nslot + RIM, :] = jnp.where(
        g > 0, hbuf[nslot : nslot + RIM, :].astype(F32), 0.0
    ).astype(BF16)
    hbuf[nslot + RIM : nslot + 2 * RIM, :] = jnp.where(
        g < ng - 1, hbuf[nslot + RIM : nslot + 2 * RIM, :].astype(F32), 0.0
    ).astype(BF16)
    grad_x[...] += nn(ohs[...], hbuf[...])

    arrived(16, wbuf2.at[0 : nd - 1])
    wout[...] = jnp.sum(wbuf2[...], axis=0)
    to_group(17, lambda q: wout, rows(wtab, g * wb, wb))
    rows(wtab, g * wb, wb)[...] = wout[...]
    arrived(17, wtab.at[0 : (ng - 1) * wb])
    grad_w[...] = wtab[...]

    for ph, ref in waits:
        pltpu.make_async_copy(ref, ref, ssem.at[ph]).wait()


def solution(mesh):
    ng, nd = mesh.shape["group"], mesh.shape["dom"]
    nslot = nd * SLOT
    ext_rows = NODE + nslot + 2 * RIM
    c_rows = NC + nslot
    tb, wb = NCC // nd, H // ng

    def local(
        features, cotangent, fine_send, fine_rim, fine_src, fine_dst, fine_pool,
        coarse_send, coarse_src, coarse_dst, coarse_pool,
        w_send, w_recv, w_node, v_send, v_recv, v_node, w_top,
    ):
        far = coarse_src - NC
        csrc = jnp.where(far < 0, coarse_src, NC + (far // CSLOT) * SLOT + far % CSLOT)
        csend = jnp.pad(coarse_send, ((0, 0), (0, SLOT - CSLOT)), constant_values=NC)
        cpool = jnp.tile(coarse_pool, 128 // NC)
        idx = jnp.concatenate(
            [
                fine_src, fine_dst, fine_pool, fine_send.reshape(-1), fine_rim.reshape(-1),
                csend.reshape(-1), csrc, coarse_dst, cpool,
                jnp.zeros((R_ALL - R_CPOOL - 1) * 128, jnp.int32),
            ]
        ).reshape(R_ALL, 128)
        vm = pl.BlockSpec(memory_space=pltpu.VMEM)
        return pl.pallas_call(
            functools.partial(kernel, ng, nd),
            out_shape=(
                jax.ShapeDtypeStruct((NODE, H), BF16),
                jax.ShapeDtypeStruct((NODE, H), F32),
                jax.ShapeDtypeStruct((H, H), F32),
            ),
            in_specs=[vm] * 10,
            out_specs=(vm, vm, vm),
            scratch_shapes=[
                pltpu.VMEM((EDGE // BLK, ext_rows + NODE, BLK), BF16),
                pltpu.VMEM((nd * NC, NODE), BF16),
                pltpu.VMEM((NODE, nd * NC), BF16),
                pltpu.VMEM((NODE, nslot + 2 * RIM), BF16),
                pltpu.VMEM((c_rows + NC, CEDGE), BF16),
                pltpu.VMEM((EDGE // BLK, H, BLK), F32),
                pltpu.VMEM((ext_rows + NODE, H), F32),
                pltpu.VMEM((ext_rows, H), BF16),
                pltpu.VMEM((H, ext_rows + NODE), BF16),
                pltpu.VMEM((nslot + 2 * RIM, H), BF16),
                pltpu.VMEM((nd * NC, H), BF16),
                pltpu.VMEM((nd, NC, H), BF16),
                pltpu.VMEM((nd * NC, H), BF16),
                pltpu.VMEM((nd, NC, H), BF16),
                pltpu.VMEM((nslot, H), BF16),
                pltpu.VMEM((c_rows, H), BF16),
                pltpu.VMEM((NCC, H), BF16),
                pltpu.VMEM((nd, tb, H), BF16),
                pltpu.VMEM((NCC, H), BF16),
                pltpu.VMEM((nd, tb, H), BF16),
                pltpu.VMEM((tb, H), F32),
                pltpu.VMEM((ng, tb, H), F32),
                pltpu.VMEM((tb, H), F32),
                pltpu.VMEM((ng, tb, H), F32),
                pltpu.VMEM((2 * tb, H), BF16),
                pltpu.VMEM((2 * NCC, H), BF16),
                pltpu.VMEM((NC, H), BF16),
                pltpu.VMEM((nd * NC, H), BF16),
                pltpu.VMEM((nslot, H), BF16),
                pltpu.VMEM((nslot, H), BF16),
                pltpu.VMEM((NC, H), BF16),
                pltpu.VMEM((nd * NC, H), BF16),
                pltpu.VMEM((nslot + 2 * RIM, H), BF16),
                pltpu.VMEM((nslot + 2 * RIM, H), BF16),
                pltpu.VMEM((H, H), F32),
                pltpu.VMEM((ng, wb, H), F32),
                pltpu.VMEM((wb, H), F32),
                pltpu.VMEM((nd, wb, H), F32),
                pltpu.VMEM((wb, H), F32),
                pltpu.VMEM((H, H), F32),
                pltpu.SemaphoreType.DMA((18,)),
                pltpu.SemaphoreType.DMA((18,)),
            ],
            compiler_params=pltpu.CompilerParams(
                collective_id=0, has_side_effects=True, vmem_limit_bytes=60 * 1024 * 1024
            ),
        )(features, cotangent, idx, w_send, w_recv, w_node, v_send, v_recv, v_node, w_top)

    both = P(("group", "dom"))
    rows = P(("group", "dom"), None)
    in_specs = (rows, rows, rows, rows, both, both, both, rows, both, both, both) + (P(),) * 7
    return jax.shard_map(
        local, mesh=mesh, in_specs=in_specs, out_specs=(rows, rows, P()), check_vma=False
    )
```

time: 361 us -> 99.3 us (0.28)
  other arithmetic: 99.8 us -> 0.02 us
  Pallas kernels: 0 us -> 88 us
  starting transfers between devices: 84.1 us -> 0 us
  waiting for transfers between devices: 69.6 us -> 0 us
  local copies, waits for them, and re-layouts: 63.1 us -> 10.2 us
  blocking collectives: 30.1 us -> 0 us
  matrix products: 10.9 us -> 0 us
    scatter-add x13 -> x0, other arithmetic: 89.3 us -> none  [the longest x2 25.2 us: edge_forward(): jax.ops.segment_sum(message.astype(jnp.float32), targets, num_segments=ow...]
    pallas_call x0 -> x1, Pallas kernels: none -> 88 us  [local(): pl.pallas_call(functools.partial(kernel, ng, nd), out_shape=(jax.ShapeDty...]
    all_to_all x14 -> x0, starting transfers between devices: 72.6 us -> none  [the longest x6 29.1 us: sent_to_all(): return lax.all_to_all(copies, axis, split_axis=0, concat_axis=0, tiled=True)]
    all_to_all x14 -> x0, waiting for transfers between devices: 69.6 us -> none  [the longest x6 30.5 us: sent_to_all(): return lax.all_to_all(copies, axis, split_axis=0, concat_axis=0, tiled=True)]
    gather x13 -> x0, local copies, waits for them, and re-layouts: 50.1 us -> none  [the longest x2 14.9 us: edge_backward(): grad_pre = (grad_sum[targets] * silu_slope(preact)).astype(jnp.bfloat16)]
    all_to_all x2 -> x0, blocking collectives: 30.1 us -> none  [the longest x1 17.9 us: sum_by_axis(): return jnp.sum(lax.all_to_all(own, far, 0, 0, tiled=True), axis=0)]
    ppermute x4 -> x0, starting transfers between devices: 11.6 us -> none  [the longest x2 8.98 us: with_halo(): lax.ppermute(lax.slice_in_dim(block, block.shape[dim] - width, None, axis...]
    dot_general x15 -> x0, matrix products: 10.9 us -> none  [the longest x2 2.67 us: edge_forward(): jnp.dot(own_rows[targets], w_recv, preferred_element_type=jnp.float32)]
  transfers between devices with their start and end apart: 18 -> 0, of which waited for: 10 -> 0; matrix products, arithmetic and copies ran while one was open for 30% -> 0% of each run, Pallas kernels for 0% -> 0%
where the time goes in v1:
time: 99.3 us; the launch traced here: 98.9 us
  Pallas kernels  88 us (89%)
  local copies, waits for them, and re-layouts  10.2 us (10%)
    pallas_call x1, Pallas kernels, local(): pl.pallas_call(functools.partial(kernel, ng, nd), out_shape=(jax.ShapeDty...  88 us
    unnamed x33, local copies, waits for them, and re-layouts  9.25 us

profile of v1, /device:TPU:1, one launch (start us, length us, event | category | flops | bytes accessed | tf_op | source)
XLA Modules:
  0.0 98.9 jit_solution(6706987326580712079)
XLA Ops:
  0.6 0.7 tile.4
  1.3 0.1 tile.10
  1.4 0.8 copy.21
  2.1 0.0 copy-start.5
  2.1 0.1 reshape.19
  2.2 0.6 copy-done.5
  2.8 0.1 copy.23
  2.9 0.0 copy-start.3
  2.9 0.1 reshape.21
  3.0 0.6 copy-done.3
  3.6 0.7 copy-done.4
  4.4 0.7 copy-done.6
  5.1 0.7 copy-done.7
  5.7 0.7 copy-done.8
  6.4 0.7 copy-done.9
  7.1 0.0 copy-start.1
  7.1 0.6 copy-done.1
  7.7 88.0 %shard_map.193 = (bf16[512,128]{1,0:T(8,128)(2,1)}, f32[512,128]{1,0:T(8,128)}, f32[128,128]{1,0:T(8,128)}) custom-call(bf16[512,128]{1,0:T(8,128)(2,1)} %feat.1, bf16[512,128]{1,0:T(8,128)(2,1)} %cot.1, s32[88,128]{1,0:T(8,128)} %bitcast.3, bf16[128,128]{1,0:T(8,128)(2,1)} %w_send.1, bf16[128,128]{1,0:T(8,128)(2,1)} %w_recv.1, bf16[128,128]{1,0:T(8,128)(2,1)} %w_node.1, ...), custom_call_target="tpu_custom_call" | custom-call | tf_op jit(solution)/shard_map/pallas_call | solution.py:352
  95.8 0.0 copy-start
  95.8 1.6 %copy.36 = bf16[512,128]{1,0:T(8,128)(2,1)} copy(bf16[512,128]{1,0:T(8,128)(2,1)} %get-tuple-element.6) | data formatting | bytes 262144
  97.4 0.0 copy-done
  97.4 0.7 copy.37
  98.1 0.2 copy-done.2
  98.2 0.6 copy.38
  (17 shorter events, 0.1 us)
Async XLA Ops:
  2.1 0.7 copy-start.5
  2.9 0.7 copy-start.3
  3.6 0.7 copy-start.4
  4.4 0.7 copy-start.6
  5.0 0.7 copy-start.7
  5.7 0.7 copy-start.8
  6.4 0.7 copy-start.9
  7.1 0.6 copy-start.1
  95.8 1.6 %copy-start = (f32[512,128]{1,0:T(8,128)S(1)}, f32[512,128]{1,0:T(8,128)}, u32[]{:S(2)}) copy-start(f32[512,128]{1,0:T(8,128)} %get-tuple-element.7) | copy-start | bytes 786436
  97.4 0.9 copy-start.2

commit v2 on v1

v2 whole, which is shorter than its diff:
```python
import functools

import jax
import jax.numpy as jnp
from jax import lax
from jax.experimental import pallas as pl
from jax.experimental.pallas import tpu as pltpu
from jax.sharding import PartitionSpec as P

F32 = jnp.float32
BF16 = jnp.bfloat16
I32 = jnp.int32
MESH = pl.DeviceIdType.MESH

H = 128
NODE = 512
EDGE = 4096
SLOT = 16
RIM = 128
NC = 32
CEDGE = 256
CSLOT = 4
BLK = 1024
NB = EDGE // BLK

(A, RZ, IX, IZ, GB, PB, GA, CH, ZG, MA, ZT, CR, GC, CO, W1, HR, HZ, W2, W3) = range(19)


def nn(a, b):
    return jnp.dot(a, b, preferred_element_type=F32)


def nt(a, b):
    return lax.dot_general(a, b, (((1,), (1,)), ((), ())), preferred_element_type=F32)


def one_where(mask):
    return jnp.where(mask, 1.0, 0.0).astype(BF16)


def hot_rows(count, row):
    return one_where(lax.broadcasted_iota(I32, (count, 128), 0) == row)


def down(row):
    return jnp.transpose(jnp.broadcast_to(row, (128, 128)))


def hot_cols(count, row):
    idx = down(row)
    at = lax.broadcasted_iota(I32, (128, 128), 1)
    parts = [one_where(at + 128 * m == idx) for m in range(count // 128)]
    return jnp.concatenate(parts, axis=1) if len(parts) > 1 else parts[0]


def gate(v):
    return 0.5 + 0.5 * jnp.tanh(0.5 * v)


def turned(w):
    return jnp.transpose(w.astype(F32)).astype(BF16)


def kernel(
    ng, nd, *refs,
):
    n_in = 18
    hbm = refs[:n_in]
    flow, grad_x, grad_w = refs[n_in : n_in + 3]
    vin = refs[n_in + 3 : 2 * n_in + 3]
    (
        oht, ohp, ohpr, ohs, ohc, ohcs, quest, slope, gpre, srcs, sacc, ext, zt, wide,
        out_a, cp_out, cp_all, cp_z, gsend, gbuf, psend, pbuf, gcout, gctab, csend, cext,
        zgsend, zgbuf, mout, mtab, zsend, zbuf, fsend, fbuf, gout, gtab, eout, etab,
        wsend, wbuf, wmid, wbuf2, wout, wtab, hsend, hbuf, isem, ssem, rsem,
    ) = refs[2 * n_in + 3 :]
    (
        feat, cot, f_send, f_rim, f_src, f_dst, f_pool, c_send, c_src, c_dst, c_pool,
        w_send, w_recv, w_node, v_send, v_recv, v_node, w_top,
    ) = vin

    g = lax.axis_index("group")
    d = lax.axis_index("dom")

    barrier = pltpu.get_barrier_semaphore()

    def greet_dom(j, c):
        pl.semaphore_signal(barrier, inc=1, device_id=(g, lax.rem(d + j, nd)), device_id_type=MESH)
        return c

    def greet_group(j, c):
        pl.semaphore_signal(barrier, inc=1, device_id=(lax.rem(g + j, ng), d), device_id_type=MESH)
        return c

    order = (0, 2, 3, 10, 4, 5, 6, 1, 11, 12, 7, 8, 9, 13, 14, 15, 16, 17)
    for i in order:
        pltpu.make_async_copy(hbm[i], vin[i], isem.at[i]).start()
    lax.fori_loop(1, nd, greet_dom, 0)
    lax.fori_loop(1, ng, greet_group, 0)

    def fetched(*which):
        for i in which:
            pltpu.make_async_copy(hbm[i], vin[i], isem.at[i]).wait()

    def push(ph, src, dst, device):
        pltpu.make_async_remote_copy(
            src_ref=src, dst_ref=dst, send_sem=ssem.at[ph], recv_sem=rsem.at[ph],
            device_id=device, device_id_type=MESH,
        ).start()

    def to_dom(ph, src, dst):
        def step(j, c):
            p = lax.rem(d + j, nd)
            push(ph, src(p), dst, (g, p))
            return c

        lax.fori_loop(nd // 2, nd, step, 0)
        lax.fori_loop(1, nd // 2, step, 0)

    def to_group(ph, src, dst):
        def step(j, c):
            q = lax.rem(g + j, ng)
            push(ph, src(q), dst, (q, d))
            return c

        lax.fori_loop(ng // 2, ng, step, 0)
        lax.fori_loop(1, ng // 2, step, 0)

    waits = []

    def arrived(ph, ref):
        pltpu.make_async_copy(ref, ref, rsem.at[ph]).wait()
        waits.append((ph, ref))

    def rows(ref, at, count):
        return ref.at[pl.ds(pl.multiple_of(at, 8), count)]

    lane = lax.broadcasted_iota(I32, (1, 128), 1)
    nslot = nd * SLOT
    halo = nslot + 2 * RIM
    own = 2 * NODE
    total = own + halo
    c_rows = NC + nslot
    prev, nxt = lax.rem(g + ng - 1, ng), lax.rem(g + 1, ng)

    def flat(ref, count, fill):
        wide[0:SLOT, :] = jnp.full((SLOT, 128), fill, I32)
        wide[0:count, 0:nd] = ref[...]
        t = jnp.transpose(wide[...])[0:nd, :]
        for s in (SLOT, 2 * SLOT, 4 * SLOT):
            t = t + pltpu.roll(t, s, 1)
        at = lax.broadcasted_iota(I32, (nd, 128), 0) & 7
        t = jnp.where(lax.broadcasted_iota(I32, (nd, 128), 1) // SLOT == at, t, 0)
        return [
            jnp.sum(t[8 * k : 8 * k + 8, :], axis=0, keepdims=True) for k in range(nslot // 128)
        ]

    wide[...] = jnp.zeros_like(wide)
    fetched(0, 2, 3, 10)
    x = feat[...]
    send_rows = flat(f_send, SLOT, 0) + [f_rim[0:1, :], f_rim[1:2, :]]
    for k, row in enumerate(send_rows):
        out_a[128 * k : 128 * k + 128, :] = nn(hot_cols(NODE, row), x).astype(BF16)
    cp = jnp.concatenate([c_pool[...]] * (128 // NC), axis=1)
    cp_out[...] = cp

    pl.semaphore_wait(barrier, nd - 1 + ng - 1)
    to_dom(A, lambda p: rows(out_a, p * SLOT, SLOT), rows(ext, NODE + d * SLOT, SLOT))
    push(RZ, out_a.at[nslot : nslot + RIM], ext.at[NODE + nslot + RIM : NODE + halo], (prev, d))
    push(RZ, out_a.at[nslot + RIM : halo], ext.at[NODE + nslot : NODE + nslot + RIM], (nxt, d))
    to_group(IZ, lambda q: cp_out, cp_z.at[g])
    to_dom(IX, lambda p: cp_out, cp_all.at[d])
    rows(ext, NODE + d * SLOT, SLOT)[...] = rows(out_a, d * SLOT, SLOT)[...]
    cp_all[d] = cp
    cp_z[g] = cp
    ext[0:NODE, :] = x

    fetched(4, 5)

    def build(b, c):
        for r in range(BLK // 128):
            src = f_src[pl.ds(b * (BLK // 128) + r, 1), :]
            dst = f_dst[pl.ds(b * (BLK // 128) + r, 1), :]
            oht[b, 0:NODE, 128 * r : 128 * r + 128] = hot_rows(NODE, dst)
            oht[b, NODE:total, 128 * r : 128 * r + 128] = hot_rows(total - NODE, src)
        return c

    lax.fori_loop(0, NB, build, 0)

    fetched(11, 12)
    ws_t, wr_t = turned(w_send[...]), turned(w_recv[...])
    zt[:, 0:NODE] = nt(wr_t, x).astype(BF16)
    zt[:, NODE:own] = nt(ws_t, x).astype(BF16)

    def begin(b, c):
        slope[b] = nn(zt[:, 0:own], oht[b, 0:own, :])
        return c

    lax.fori_loop(0, NB, begin, 0)

    fetched(6, 1)
    for k in range(NODE // 128):
        row = f_pool[k : k + 1, :]
        ohp[:, 128 * k : 128 * k + 128] = hot_rows(nd * NC, row)
    gsend[...] = nn(ohp[...], cot[...]).astype(BF16)
    fetched(7, 8, 9, 13, 14, 15, 16, 17)

    arrived(A, ext.at[0 : (nd - 1) * SLOT])
    arrived(RZ, ext.at[0 : 2 * RIM])
    at = NODE + nslot
    ext[at : at + RIM, :] = jnp.where(g > 0, ext[at : at + RIM, :].astype(F32), 0.0).astype(BF16)
    ext[at + RIM : at + 2 * RIM, :] = jnp.where(
        g < ng - 1, ext[at + RIM : at + 2 * RIM, :].astype(F32), 0.0
    ).astype(BF16)
    zt[:, own:total] = nt(ws_t, ext[NODE : NODE + halo, :]).astype(BF16)
    to_dom(GB, lambda p: rows(gsend, p * NC, NC), gbuf.at[d])
    gbuf[d] = rows(gsend, d * NC, NC)[...]
    sacc[0:NODE, :] = jnp.zeros((NODE, H), F32)

    def forward(b, c):
        pre = slope[b] + nn(zt[:, own:total], oht[b, own:total, :])
        s = gate(pre)
        slope[b] = s * (1.0 + pre * (1.0 - s))
        msg = (pre * s).astype(BF16)
        sacc[0:NODE, :] += nt(oht[b, 0:NODE, :], msg)
        return c

    lax.fori_loop(0, NB, forward, 0)
    updated = (x.astype(F32) + nn(sacc[0:NODE, :].astype(BF16), w_node[...])).astype(BF16)
    psend[...] = nn(ohp[...], updated).astype(BF16)
    to_dom(PB, lambda p: rows(psend, p * NC, NC), pbuf.at[d])
    pbuf[d] = rows(psend, d * NC, NC)[...]

    arrived(GB, gbuf.at[0 : nd - 1])
    grad_coarse = jnp.sum(gbuf[...].astype(F32), axis=0)
    gcout[...] = grad_coarse.astype(BF16)
    to_dom(GA, lambda p: gcout, rows(gctab, d * NC, NC))
    rows(gctab, d * NC, NC)[...] = gcout[...]

    send_c = flat(c_send, CSLOT, NC)
    for k, row in enumerate(send_c):
        ohcs[:, 128 * k : 128 * k + 128] = hot_rows(NC, row)
    for k in range(CEDGE // 128):
        src = c_src[k : k + 1, :]
        far = src - NC
        src = jnp.where(far < 0, src, NC + (far >> 2) * SLOT + (far & 3))
        ohc[0:c_rows, 128 * k : 128 * k + 128] = hot_rows(c_rows, src)
        ohc[c_rows : c_rows + NC, 128 * k : 128 * k + 128] = hot_rows(NC, c_dst[k : k + 1, :])
    outs_c = [hot_cols(128, row)[:, 0:NC] for row in send_c]
    vs_t, vr_t = turned(v_send[...]), turned(v_recv[...])

    arrived(PB, pbuf.at[0 : nd - 1])
    coarse_in = (0.25 * jnp.sum(pbuf[...].astype(F32), axis=0)).astype(BF16)
    for k in range(nslot // 128):
        csend[128 * k : 128 * k + 128, :] = nn(outs_c[k], coarse_in).astype(BF16)
    to_dom(CH, lambda p: rows(csend, p * SLOT, SLOT), rows(cext, NC + d * SLOT, SLOT))
    cext[0:NC, :] = coarse_in
    rows(cext, NC + d * SLOT, SLOT)[...] = rows(csend, d * SLOT, SLOT)[...]

    arrived(IX, cp_all.at[0 : nd - 1])
    arrived(IZ, cp_z.at[0 : ng - 1])

    def joined(ref, k):
        row = ref[4 * k]
        for a in range(1, 4):
            row = jnp.where(lane // NC == a, ref[4 * k + a], row)
        return row

    for k in range(ng * NC // 128):
        want = down(joined(cp_z, k))
        for m in range(nd * NC // 128):
            quest[128 * k : 128 * k + 128, 128 * m : 128 * m + 128] = one_where(
                want == joined(cp_all, m)
            )

    arrived(GA, gctab.at[0 : (nd - 1) * NC])
    zgsend[...] = nn(quest[...], gctab[...]).astype(BF16)
    to_group(ZG, lambda q: rows(zgsend, q * NC, NC), zgbuf.at[g])
    zgbuf[g] = rows(zgsend, g * NC, NC)[...]

    arrived(CH, cext.at[0 : (nd - 1) * SLOT])
    cz = jnp.concatenate(
        [nt(vs_t, cext[...]).astype(BF16), nt(vr_t, coarse_in).astype(BF16)], axis=1
    )
    cpre = nn(cz, ohc[...])
    cs = gate(cpre)
    cslope = cs * (1.0 + cpre * (1.0 - cs))
    csum = nt(ohc[c_rows : c_rows + NC, :], (cpre * cs).astype(BF16))
    coarse_mid = coarse_in.astype(F32) + nn(csum.astype(BF16), v_node[...])
    mout[...] = coarse_mid.astype(BF16)
    to_dom(MA, lambda p: mout, rows(mtab, d * NC, NC))
    rows(mtab, d * NC, NC)[...] = mout[...]
    coarse_mid = mout[...].astype(F32)

    ext_t = jnp.transpose(ext[...].astype(F32)).astype(BF16)

    def pick(b, c):
        srcs[b] = nn(ext_t, oht[b, NODE:total, :]).astype(BF16)
        return c

    lax.fori_loop(0, NB, pick, 0)
    arrived(ZG, zgbuf.at[0 : ng - 1])
    grad_top = jnp.sum(zgbuf[...].astype(F32), axis=0)

    arrived(MA, mtab.at[0 : (nd - 1) * NC])
    zsend[...] = nn(quest[...], mtab[...]).astype(BF16)
    to_group(ZT, lambda q: rows(zsend, q * NC, NC), zbuf.at[g])
    zbuf[g] = rows(zsend, g * NC, NC)[...]
    for k in range(NODE // 128):
        ohpr[128 * k : 128 * k + 128, :] = hot_cols(nd * NC, f_pool[k : k + 1, :])
    arrived(ZT, zbuf.at[0 : ng - 1])
    pooled = 0.125 * jnp.sum(zbuf[...].astype(F32), axis=0)
    slope_in = nn(pooled.astype(BF16), w_top[...])
    ts = gate(slope_in)
    top_out = (pooled + slope_in * ts).astype(BF16)
    inner = (grad_top * (ts * (1.0 + slope_in * (1.0 - ts)))).astype(BF16)
    grad_pool = grad_top + nt(inner, w_top[...])

    grad_cmid = grad_coarse + 0.125 * grad_pool
    cgs = nt(v_node[...], grad_cmid.astype(BF16)).astype(BF16)
    cgp = (nn(cgs, ohc[c_rows : c_rows + NC, :]) * cslope).astype(BF16)
    csc = nt(ohc[...], cgp).astype(BF16)
    cge = nt(csc[0:c_rows, :], v_send[...])
    fsend[...] = cge[NC:c_rows, :].astype(BF16)
    to_dom(CR, lambda p: rows(fsend, p * SLOT, SLOT), rows(fbuf, d * SLOT, SLOT))
    rows(fbuf, d * SLOT, SLOT)[...] = rows(fsend, d * SLOT, SLOT)[...]
    c_own = grad_cmid + nt(csc[c_rows : c_rows + NC, :], v_recv[...]) + cge[0:NC, :]
    for k, row in enumerate(send_rows):
        ohs[:, 128 * k : 128 * k + 128] = hot_rows(NODE, row)
    eout[...] = (coarse_mid + top_out.astype(F32)).astype(BF16)
    arrived(CR, fbuf.at[0 : (nd - 1) * SLOT])
    gout[...] = (c_own + nn(ohcs[...], fbuf[...])).astype(BF16)
    to_dom(GC, lambda p: gout, rows(gtab, d * NC, NC))
    rows(gtab, d * NC, NC)[...] = gout[...]

    arrived(GC, gtab.at[0 : (nd - 1) * NC])
    to_dom(CO, lambda p: eout, rows(etab, d * NC, NC))
    rows(etab, d * NC, NC)[...] = eout[...]
    grad_mid = cot[...].astype(F32) + 0.25 * nn(ohpr[...], gtab[...])
    gs = nt(w_node[...], grad_mid.astype(BF16)).astype(BF16)

    def edges(b, acc):
        gp = (nn(gs, oht[b, 0:NODE, :]) * slope[b]).astype(BF16)
        gpre[b] = gp
        return acc + nt(srcs[b], gp)

    wb = H // ng
    wsend[...] = lax.fori_loop(0, NB, edges, jnp.zeros((H, H), F32)).astype(BF16)
    to_group(W1, lambda q: rows(wsend, q * wb, wb), wbuf.at[g])
    wbuf[g] = rows(wsend, g * wb, wb)[...]

    sacc[...] = jnp.zeros_like(sacc)

    def back_halo(b, c):
        sacc[own:total, :] += nt(oht[b, own:total, :], gpre[b])
        return c

    lax.fori_loop(0, NB, back_halo, 0)
    hsend[...] = nt(sacc[own:total, :].astype(BF16), w_send[...]).astype(BF16)
    to_dom(HR, lambda p: rows(hsend, p * SLOT, SLOT), rows(hbuf, d * SLOT, SLOT))
    push(HZ, hsend.at[nslot : nslot + RIM], hbuf.at[nslot + RIM : halo], (prev, d))
    push(HZ, hsend.at[nslot + RIM : halo], hbuf.at[nslot : nslot + RIM], (nxt, d))
    rows(hbuf, d * SLOT, SLOT)[...] = rows(hsend, d * SLOT, SLOT)[...]

    arrived(W1, wbuf.at[0 : ng - 1])
    wmid[...] = jnp.sum(wbuf[...].astype(F32), axis=0).astype(BF16)
    to_dom(W2, lambda p: wmid, wbuf2.at[d])
    wbuf2[d] = wmid[...]

    def back_own(b, c):
        sacc[0:own, :] += nt(oht[b, 0:own, :], gpre[b])
        return c

    lax.fori_loop(0, NB, back_own, 0)
    s_own = sacc[0:own, :].astype(BF16)
    grad_x[...] = grad_mid + nt(s_own[0:NODE, :], w_recv[...]) + nt(s_own[NODE:own, :], w_send[...])
    arrived(CO, etab.at[0 : (nd - 1) * NC])
    flow[...] = (updated.astype(F32) + nn(ohpr[...], etab[...])).astype(BF16)

    arrived(W2, wbuf2.at[0 : nd - 1])
    wout[...] = jnp.sum(wbuf2[...].astype(F32), axis=0)
    to_group(W3, lambda q: wout, rows(wtab, g * wb, wb))
    rows(wtab, g * wb, wb)[...] = wout[...]

    arrived(HR, hbuf.at[0 : (nd - 1) * SLOT])
    arrived(HZ, hbuf.at[0 : 2 * RIM])
    hbuf[nslot : nslot + RIM, :] = jnp.where(
        g > 0, hbuf[nslot : nslot + RIM, :].astype(F32), 0.0
    ).astype(BF16)
    hbuf[nslot + RIM : halo, :] = jnp.where(
        g < ng - 1, hbuf[nslot + RIM : halo, :].astype(F32), 0.0
    ).astype(BF16)
    grad_x[...] += nn(ohs[...], hbuf[...])

    for ph, ref in waits:
        pltpu.make_async_copy(ref, ref, ssem.at[ph]).wait()
    arrived(W3, wtab.at[0 : (ng - 1) * wb])
    grad_w[...] = wtab[...]
    pltpu.make_async_copy(waits[-1][1], waits[-1][1], ssem.at[W3]).wait()


def write_out(*refs):
    sem = refs[-1]
    copies = [pltpu.make_async_copy(refs[i], refs[3 + i], sem.at[i]) for i in range(3)]
    for c in copies:
        c.start()
    for c in copies:
        c.wait()


def solution(mesh):
    ng, nd = mesh.shape["group"], mesh.shape["dom"]
    nslot = nd * SLOT
    halo = nslot + 2 * RIM
    total = 2 * NODE + halo
    c_rows = NC + nslot
    wb = H // ng
    pooled = nd * NC

    def local(
        features, cotangent, fine_send, fine_rim, fine_src, fine_dst, fine_pool,
        coarse_send, coarse_src, coarse_dst, coarse_pool,
        w_send, w_recv, w_node, v_send, v_recv, v_node, w_top,
    ):
        args = (
            features, cotangent, fine_send.T, fine_rim,
            fine_src.reshape(-1, 128), fine_dst.reshape(-1, 128), fine_pool.reshape(-1, 128),
            coarse_send.T, coarse_src.reshape(-1, 128), coarse_dst.reshape(-1, 128),
            coarse_pool.reshape(1, -1),
            w_send, w_recv, w_node, v_send, v_recv, v_node, w_top,
        )
        scratch = [pltpu.VMEM(a.shape, a.dtype) for a in args] + [
            pltpu.VMEM((NB, total, BLK), BF16),
            pltpu.VMEM((pooled, NODE), BF16),
            pltpu.VMEM((NODE, pooled), BF16),
            pltpu.VMEM((NODE, halo), BF16),
            pltpu.VMEM((c_rows + NC, CEDGE), BF16),
            pltpu.VMEM((NC, nslot), BF16),
            pltpu.VMEM((ng * NC, pooled), BF16),
            pltpu.VMEM((NB, H, BLK), F32),
            pltpu.VMEM((NB, H, BLK), BF16),
            pltpu.VMEM((NB, H, BLK), BF16),
            pltpu.VMEM((total, H), F32),
            pltpu.VMEM((NODE + halo, H), BF16),
            pltpu.VMEM((H, total), BF16),
            pltpu.VMEM((128, 128), I32),
            pltpu.VMEM((halo, H), BF16),
            pltpu.VMEM((1, 128), I32),
            pltpu.VMEM((nd, 1, 128), I32),
            pltpu.VMEM((ng, 1, 128), I32),
            pltpu.VMEM((pooled, H), BF16),
            pltpu.VMEM((nd, NC, H), BF16),
            pltpu.VMEM((pooled, H), BF16),
            pltpu.VMEM((nd, NC, H), BF16),
            pltpu.VMEM((NC, H), BF16),
            pltpu.VMEM((pooled, H), BF16),
            pltpu.VMEM((nslot, H), BF16),
            pltpu.VMEM((c_rows, H), BF16),
            pltpu.VMEM((ng * NC, H), BF16),
            pltpu.VMEM((ng, NC, H), BF16),
            pltpu.VMEM((NC, H), BF16),
            pltpu.VMEM((pooled, H), BF16),
            pltpu.VMEM((ng * NC, H), BF16),
            pltpu.VMEM((ng, NC, H), BF16),
            pltpu.VMEM((nslot, H), BF16),
            pltpu.VMEM((nslot, H), BF16),
            pltpu.VMEM((NC, H), BF16),
            pltpu.VMEM((pooled, H), BF16),
            pltpu.VMEM((NC, H), BF16),
            pltpu.VMEM((pooled, H), BF16),
            pltpu.VMEM((H, H), BF16),
            pltpu.VMEM((ng, wb, H), BF16),
            pltpu.VMEM((wb, H), BF16),
            pltpu.VMEM((nd, wb, H), BF16),
            pltpu.VMEM((wb, H), F32),
            pltpu.VMEM((H, H), F32),
            pltpu.VMEM((halo, H), BF16),
            pltpu.VMEM((halo, H), BF16),
            pltpu.SemaphoreType.DMA((len(args),)),
            pltpu.SemaphoreType.DMA((19,)),
            pltpu.SemaphoreType.DMA((19,)),
        ]
        vm = pl.BlockSpec(memory_space=pltpu.VMEM)
        anywhere = pl.BlockSpec(memory_space=pl.ANY)
        shapes = (((NODE, H), BF16), ((NODE, H), F32), ((H, H), F32))
        parts = pl.pallas_call(
            functools.partial(kernel, ng, nd),
            out_shape=tuple(pltpu.VMEM(s, t) for s, t in shapes),
            in_specs=[anywhere] * len(args),
            out_specs=(vm, vm, vm),
            scratch_shapes=scratch,
            compiler_params=pltpu.CompilerParams(
                collective_id=0, has_side_effects=True, vmem_limit_bytes=58 * 1024 * 1024
            ),
        )(*args)
        return pl.pallas_call(
            write_out,
            out_shape=tuple(jax.ShapeDtypeStruct(s, t) for s, t in shapes),
            in_specs=[vm, vm, vm],
            out_specs=(anywhere, anywhere, anywhere),
            scratch_shapes=[pltpu.SemaphoreType.DMA((3,))],
        )(*[pltpu.with_memory_space_constraint(p, pltpu.VMEM) for p in parts])

    both = P(("group", "dom"))
    rows = P(("group", "dom"), None)
    in_specs = (rows, rows, rows, rows, both, both, both, rows, both, both, both) + (P(),) * 7
    return jax.shard_map(
        local, mesh=mesh, in_specs=in_specs, out_specs=(rows, rows, P()), check_vma=False
    )
```

time: 99.3 us -> 78.2 us (0.79)
  Pallas kernels: 88 us -> 77.5 us
  local copies, waits for them, and re-layouts: 10.2 us -> 0 us
    pallas_call x1 -> x2, Pallas kernels: 88 us -> 77.5 us  [the longest x1 76.7 us: local(): pl.pallas_call(functools.partial(kernel, ng, nd), out_shape=tuple((pltpu....]
    unnamed x33 -> x0, local copies, waits for them, and re-layouts: 9.25 us -> none
where the time goes in v2:
time: 78.2 us; the launch traced here: 78.1 us
  Pallas kernels  77.5 us (99%)
    pallas_call x1, Pallas kernels, local(): pl.pallas_call(functools.partial(kernel, ng, nd), out_shape=tuple((pltpu....  76.7 us

profile of v2, /device:TPU:1, one launch (start us, length us, event | category | flops | bytes accessed | tf_op | source)
XLA Modules:
  0.0 78.1 jit_solution(8559652444013336833)
XLA Ops:
  0.6 76.7 %shard_map.193 = (bf16[512,128]{1,0:T(8,128)(2,1)S(1)}, f32[512,128]{1,0:T(8,128)S(1)}, f32[128,128]{1,0:T(8,128)S(1)}) custom-call(bf16[512,128]{1,0:T(8,128)(2,1)} %refs_0_.1, bf16[512,128]{1,0:T(8,128)(2,1)} %refs_1_.1, s32[16,32]{1,0:T(8,128)} %bitcast.10, s32[2,128]{1,0:T(2,128)} %refs_3_.1, s32[32,128]{1,0:T(8,128)} %bitcast.8, s32[32,128]{1,0:T(8,128)} %bitcast.9, ...), custom_call_target="tpu_custom_call" | custom-call | tf_op jit(solution)/shard_map/pallas_call | solution.py:486
  77.3 0.8 %shard_map.194 = (bf16[512,128]{1,0:T(8,128)(2,1)}, f32[512,128]{1,0:T(8,128)}, f32[128,128]{1,0:T(8,128)}) custom-call(bf16[512,128]{1,0:T(8,128)(2,1)S(1)} %get-tuple-element.6.refs_0_, f32[512,128]{1,0:T(8,128)S(1)} %get-tuple-element.7.refs_1_, f32[128,128]{1,0:T(8,128)S(1)} %get-tuple-element.8.refs_2_), custom_call_target="tpu_custom_call" | custom-call | tf_op jit(solution)/shard_map/pallas_call | solution.py:496
